TPU v7x, 32 devices: a whole 2x2x4 slice. The times are simulated.
32 devices in a mesh: grp: 2 (over y), tp: 8 (over z, x), sub: 2 (over core).
Axes of the slice: x: 2, y: 2, z: 4, core: 2. Of those that a mesh axis runs over, the one named last changes fastest.
Arguments:
- hidden_in: bfloat16 [32, 2, 4096], P('grp', 'sub', 'tp'), parts along dimension 0, may hold values from -16 to 16
- norm_attn: float32 [8192], replicated, may hold values from 0.25 to 1.75
- w_query: bfloat16 [8192, 2, 4096], P(None, 'sub', 'tp'), may hold values from -0.0625 to 0.0625
- w_key: bfloat16 [8192, 2, 512], P(None, 'sub', 'tp'), may hold values from -0.0625 to 0.0625
- w_value: bfloat16 [8192, 2, 512], P(None, 'sub', 'tp'), may hold values from -0.0625 to 0.0625
- w_out: bfloat16 [2, 4096, 2, 4096], P('sub', None, None, 'tp'), may hold values from -0.0625 to 0.0625
- norm_ffn: float32 [8192], replicated, may hold values from 0.25 to 1.75
- w_gate: bfloat16 [2, 4096, 14336], P('sub', None, 'tp'), may hold values from -0.0625 to 0.0625
- w_up: bfloat16 [2, 4096, 14336], P('sub', None, 'tp'), may hold values from -0.0625 to 0.0625
- w_down: bfloat16 [14336, 2, 4096], P('tp', 'sub'), may hold values from -0.0625 to 0.0625
- cache_keys: bfloat16 [32, 64, 8, 128], P('grp', 'tp', 'sub'), parts along dimension 0, may hold values from -250 to 250
- cache_values: bfloat16 [32, 64, 8, 128], P('grp', 'tp', 'sub'), parts along dimension 0, may hold values from -6 to 6
- lengths: int32 [32], P('grp'), parts along dimension 0, may hold values from 1 to 64, as said below
Outputs:
- hidden_out: bfloat16 [32, 2, 4096], P('grp', 'sub', 'tp'), parts along dimension 0
There are 2 independent parts, one for each index of `grp`. A program takes and returns all parts, laid end to end along the dimension named above; an argument that names none is the same for every part. Nothing has to cross between parts.
Inputs may be any that keep to these rules, and one draw needn't show every extreme that they name: `lengths`: some sequence has 64 live positions and some has 1.
All inputs are finite; a program needn't handle non-finite values.
Results may differ from a plain program's by a relative error of at most 0.012.
The roundings to bfloat16 on the way count: a program that leaves them out, or rounds other values in their place, can miss the bound.
Values may be sent and summed in bfloat16 or wider, within the bound.
A program may use at most 128 MiB of HBM per device.

v0:
```python
import math
import jax
import jax.numpy as jnp
from jax import lax
from jax.sharding import PartitionSpec as P

HD = 128
epsilon = 1e-05
rope_base = 500000.0
floor_score = -1e30


def joined(part, axis, combine):
    gathered = jax.tree.map(lambda a: lax.all_gather(a, axis), part)

    def take(source):
        return jax.tree.map(lambda a: lax.dynamic_index_in_dim(a, source, 0, False), gathered)

    return lax.fori_loop(
        1, lax.axis_size(axis), lambda source, state: combine(state, take(source)), take(0)
    )


def rope_angles(lengths):
    frequencies = rope_base ** (-(jnp.arange(HD // 2, dtype=jnp.float32) * 2.0) / HD)
    return lengths.astype(jnp.float32)[:, None] * frequencies[None, :]


def rotate(vectors, angles):
    middle_index = vectors.shape[-1] // 2
    cosine = jnp.cos(angles)[:, None, :]
    sine = jnp.sin(angles)[:, None, :]
    lower = vectors[..., :middle_index]
    upper = vectors[..., middle_index:]
    return jnp.concatenate([lower * cosine - upper * sine, upper * cosine + lower * sine], axis=-1)


def spread_rows(shard):
    across = lax.all_gather(shard, "tp", axis=2, tiled=True)
    return lax.all_gather(across, "sub", axis=1, tiled=True)


def half_rows_of(shard):
    return lax.all_gather(shard, "tp", axis=2, tiled=True)


def join_partials(earlier, later):
    earlier_max, earlier_sum, earlier_out = earlier
    later_max, later_sum, later_out = later
    highest = jnp.maximum(earlier_max, later_max)
    earlier_scale = jnp.exp(earlier_max - highest)
    later_scale = jnp.exp(later_max - highest)
    joined_sum = earlier_sum * earlier_scale + later_sum * later_scale
    joined_out = earlier_out * earlier_scale[..., None] + later_out * later_scale[..., None]
    return (highest, joined_sum, joined_out)


def per_device(
    hidden_in,
    norm_attn,
    w_query,
    w_key,
    w_value,
    w_out,
    norm_ffn,
    w_gate,
    w_up,
    w_down,
    cache_keys,
    cache_values,
    lengths,
):
    seq_count = hidden_in.shape[0]
    shard_width = hidden_in.shape[2]
    half_width = shard_width * lax.axis_size("tp")
    model_width = half_width * lax.axis_size("sub")
    tp_pos = lax.axis_index("tp")
    sub_pos = lax.axis_index("sub")
    residual = hidden_in.astype(jnp.float32)
    whole_rows = spread_rows(hidden_in).astype(jnp.float32)
    factor = lax.rsqrt(jnp.mean(whole_rows * whole_rows, axis=(1, 2)) + epsilon)
    gain_whole = norm_attn.reshape(whole_rows.shape[1], half_width)
    gathered = (whole_rows * factor[:, None, None] * gain_whole).astype(jnp.bfloat16)
    flattened = gathered.reshape(seq_count, model_width)
    query_part = jnp.dot(
        flattened, w_query.reshape(model_width, -1), preferred_element_type=jnp.float32
    ).astype(jnp.bfloat16)
    key_part = jnp.dot(
        flattened, w_key.reshape(model_width, -1), preferred_element_type=jnp.float32
    ).astype(jnp.bfloat16)
    value_part = jnp.dot(
        flattened, w_value.reshape(model_width, -1), preferred_element_type=jnp.float32
    ).astype(jnp.bfloat16)
    query, key_new, value_new = (
        lax.all_gather(query_part, "tp", axis=1, tiled=True),
        lax.all_gather(key_part, "tp", axis=1, tiled=True),
        lax.all_gather(value_part, "tp", axis=1, tiled=True),
    )
    query_heads = query.shape[1] // HD
    kv_heads = key_new.shape[1] // HD
    group_size = query_heads // kv_heads
    angles = rope_angles(lengths)
    query_rot = rotate(
        query.astype(jnp.float32).reshape(seq_count, query_heads, HD), angles
    ).astype(jnp.bfloat16)
    key_rot = rotate(key_new.astype(jnp.float32).reshape(seq_count, kv_heads, HD), angles).astype(
        jnp.bfloat16
    )
    grouped = query_rot.reshape(seq_count, kv_heads, group_size, HD)
    values_new = value_new.astype(jnp.float32).reshape(seq_count, kv_heads, 1, HD)
    span = cache_keys.shape[1]
    scores = jnp.einsum(
        "bkgd,blkd->bkgl", grouped, cache_keys, preferred_element_type=jnp.float32
    ) / math.sqrt(HD)
    places = tp_pos * span + jnp.arange(span, dtype=jnp.int32)
    live = (places[None, :] < lengths[:, None])[:, None, None, :]
    masked = jnp.where(live, scores, floor_score)
    local_max = jnp.max(masked, axis=-1)
    weights = jnp.where(live, jnp.exp(masked - local_max[..., None]), 0.0)
    local_sum = jnp.sum(weights, axis=-1)
    local_out = jnp.einsum(
        "bkgl,blkd->bkgd",
        weights,
        cache_values.astype(jnp.float32),
        precision=lax.Precision.HIGHEST,
    )
    own_score = jnp.sum(
        grouped.astype(jnp.float32) * key_rot.astype(jnp.float32)[:, :, None, :], axis=-1
    ) / math.sqrt(HD)
    joined_max, joined_sum, joined_out = joined(
        (local_max, local_sum, local_out), "tp", join_partials
    )
    highest = jnp.maximum(joined_max, own_score)
    kept_scale = jnp.exp(joined_max - highest)
    own_weight = jnp.exp(own_score - highest)
    numerator = joined_out * kept_scale[..., None] + own_weight[..., None] * values_new
    denominator = joined_sum * kept_scale + own_weight
    attended = (numerator / denominator[..., None]).reshape(seq_count, -1).astype(jnp.bfloat16)
    out_part = jnp.dot(
        attended, w_out.reshape(attended.shape[1], -1), preferred_element_type=jnp.float32
    )
    out_part = out_part.reshape(seq_count, -1, shard_width)
    mixed = lax.psum_scatter(out_part, "sub", scatter_dimension=1, tiled=True)
    middle = (residual + mixed).astype(jnp.bfloat16)
    middle_float = middle.astype(jnp.float32)
    raw_half = half_rows_of(middle).astype(jnp.float32)
    partial_squares = jnp.sum(raw_half * raw_half, axis=(1, 2))
    squares_mid = lax.psum(partial_squares, "sub")
    factor_mid = lax.rsqrt(squares_mid / model_width + epsilon)
    gain_half = lax.dynamic_slice_in_dim(norm_ffn, sub_pos * half_width, half_width)
    half_rows = (raw_half * factor_mid[:, None, None] * gain_half).astype(jnp.bfloat16)
    half_flat = half_rows.reshape(seq_count, half_width)
    gate_part = jnp.dot(
        half_flat, w_gate.reshape(half_width, -1), preferred_element_type=jnp.float32
    )
    up_part = jnp.dot(half_flat, w_up.reshape(half_width, -1), preferred_element_type=jnp.float32)
    gate_total, up_total = lax.psum((gate_part, up_part), "sub")
    hidden = (jax.nn.silu(gate_total) * up_total).astype(jnp.bfloat16)
    down_part = jnp.dot(
        hidden, w_down.reshape(hidden.shape[1], -1), preferred_element_type=jnp.float32
    )
    down_total = lax.psum(down_part, "tp")
    down_share = lax.dynamic_slice_in_dim(down_total, tp_pos * shard_width, shard_width, 1)
    return (middle_float + down_share[:, None, :]).astype(jnp.bfloat16)


def solution(mesh):
    in_specs = (
        P("grp", "sub", "tp"),
        P(),
        P(None, "sub", "tp"),
        P(None, "sub", "tp"),
        P(None, "sub", "tp"),
        P("sub", None, None, "tp"),
        P(),
        P("sub", None, "tp"),
        P("sub", None, "tp"),
        P("tp", "sub", None),
        P("grp", "tp", "sub", None),
        P("grp", "tp", "sub", None),
        P("grp"),
    )
    out_specs = P("grp", "sub", "tp")
    return jax.shard_map(
        per_device, mesh=mesh, in_specs=in_specs, out_specs=out_specs, check_vma=False
    )
```

profile of v0, /device:TPU:0, one launch (start us, length us, event | category | flops | bytes accessed | tf_op | source)
XLA Modules:
  0.0 410.7 jit_solution(6426538400944346462)
XLA Ops:
  6.6 32.7 %all_gather.36 = bf16[16,1,4096]{2,0,1:T(8,128)(2,1)S(1)} all-gather(bf16[16,1,512]{2,0,1:T(8,128)(2,1)} %param.15), channel_id=1, replica_groups=mesh['grp'=2,'tp'=8,'sub'=2] {'tp'}, dimensions={2}, use_global_device_ids=true | all-gather | bytes 147456 | tf_op jit(solution)/shard_map/all_gather | solution.py:39
  39.3 2.0 all_gather.37
  41.5 0.8 mul.255
  42.4 4.6 %fusion.12 = bf16[16,512]{1,0:T(8,128)(2,1)S(1)} fusion(bf16[16,8192]{1,0:T(8,128)(2,1)S(1)} %bitcast.90, bf16[8192,1,512]{2,0,1:T(8,128)(2,1)} %param.17), kind=kOutput, calls=%fused_computation.18 | convolution fusion | flops 134225920 | bytes 8667136 | tf_op jit(solution)/shard_map/dot_general | solution.py:85
  47.0 30.5 %all_gather.38 = bf16[16,4096]{1,0:T(8,128)(2,1)S(1)} all-gather(bf16[16,512]{1,0:T(8,128)(2,1)S(1)} %fusion.12), channel_id=1, replica_groups=mesh['grp'=2,'tp'=8,'sub'=2] {'tp'}, dimensions={1}, use_global_device_ids=true | all-gather | bytes 147456 | tf_op jit(solution)/shard_map/all_gather | solution.py:95
  78.3 1.3 fusion.26
  79.9 31.0 %all-gather.1 = f32[128,4,8]{2,1,0:T(4,128)S(1)} all-gather(f32[16,4,8]{2,1,0:T(4,128)S(1)} %fusion.27), channel_id=3, replica_groups=mesh['grp'=2,'tp'=8,'sub'=2] {'tp'}, dimensions={0}, use_global_device_ids=true | all-gather | bytes 18432 | tf_op jit(solution)/shard_map/all_gather | solution.py:14
  111.1 31.7 %all-gather = f32[128,4,8]{2,1,0:T(4,128)S(1)} all-gather(f32[16,4,8]{2,1,0:T(4,128)S(1)} %get-tuple-element.236), channel_id=2, replica_groups=mesh['grp'=2,'tp'=8,'sub'=2] {'tp'}, dimensions={0}, use_global_device_ids=true | all-gather | bytes 18432 | tf_op jit(solution)/shard_map/all_gather | solution.py:14
  143.4 30.6 %all-gather.3 = bf16[8,64,16]{1,2,0:T(8,128)(2,1)S(1)} all-gather(bf16[1,64,16]{1,2,0:T(8,128)(2,1)S(1)} %fusion.15), channel_id=1, replica_groups=mesh['grp'=2,'tp'=8,'sub'=2] {'tp'}, dimensions={0}, use_global_device_ids=true | all-gather | bytes 18432 | tf_op jit(solution)/shard_map/all_gather | solution.py:96
  175.1 30.6 %all-gather.4 = bf16[8,64,16]{1,2,0:T(8,128)(2,1)S(1)} all-gather(bf16[1,64,16]{1,2,0:T(8,128)(2,1)S(1)} %fusion.16), channel_id=1, replica_groups=mesh['grp'=2,'tp'=8,'sub'=2] {'tp'}, dimensions={0}, use_global_device_ids=true | all-gather | bytes 18432 | tf_op jit(solution)/shard_map/all_gather | solution.py:97
  205.8 9.3 %copy.83 = bf16[512,8,2,512]{3,1,2,0:T(8,128)(2,1)} copy(bf16[512,8,2,512]{3,2,1,0:T(2,128)(2,1)} %bitcast.89) | data formatting | bytes 16777216
  215.1 11.4 %copy.75 = bf16[1024,4096]{1,0:T(8,128)(2,1)} copy(bf16[1024,4096]{0,1:T(8,128)(2,1)} %bitcast.88) | data formatting | bytes 16777216 | tf_op jit(solution)/shard_map/dot_general | solution.py:139
  226.5 1.0 slice.26
  227.5 10.0 %while.19 = (s32[]{:T(128)}, f32[16,4,8]{0,2,1:T(8,128)S(1)}, f32[16,4,8]{0,2,1:T(8,128)S(1)}, f32[16,4,8,128]{3,2,1,0:T(8,128)S(1)}, f32[8,16,4,8]{1,3,2,0:T(8,...) while((s32[]{:T(128)}, f32[16,4,8]{0,2,1:T(8,128)S(1)}, ...), condition=%wide.region_4.5_spmd, body=%wide.region_3.4_spmd.sunk | while | flops 199685 | bytes 815255 | solution.py:19
  227.7 1.2 fusion.58
  229.1 1.2 fusion.58
  230.5 1.2 fusion.58
  231.9 1.2 fusion.58
  233.4 1.2 fusion.58
  234.8 1.2 fusion.58
  236.2 1.2 fusion.58
  238.1 6.3 %fusion.49 = f32[16,2,512]{2,0,1:T(8,128)} fusion(bf16[16,4096,1]{1,0,2:T(8,128)(2,1)S(1)} %reshape.198, bf16[2,512,4096]{2,1,0:T(8,128)(2,1)} %bitcast.87), kind=kOutput, calls=%fused_computation.77 | convolution fusion | flops 134217728 | bytes 8585216 | tf_op jit(solution)/shard_map/dot_general | solution.py:139
  244.5 8.5 %reduce-scatter.2.cloned.1.call-done = f32[16,1,512]{2,0,1:T(8,128)} async-done(((f32[16,2,512]{2,0,1:T(8,128)}), f32[16,1,512]{2,0,1:T(8,128)}) %reduce-scatter.2.cloned.1.call-update) | async-done | bytes 32784 | tf_op jit(solution)/shard_map/reduce_scatter | solution.py:143
  253.0 0.8 add_convert_fusion.1
  253.8 30.8 %all_gather.47 = bf16[16,1,4096]{2,0,1:T(8,128)(2,1)S(1)} all-gather(bf16[16,1,512]{2,0,1:T(8,128)(2,1)S(1)} %add_convert_fusion.1), channel_id=1, replica_groups=mesh['grp'=2,'tp'=8,'sub'=2] {'tp'}, dimensions={2}, use_global_device_ids=true | all-gather | bytes 147456 | tf_op jit(solution)/shard_map/all_gather | solution.py:44
  284.7 2.6 psum.28
  287.3 7.9 %fusion.7 = f32[16,1792]{1,0:T(8,128)} fusion(bf16[1,4096,1792]{2,1,0:T(8,128)(2,1)} %param.22, bf16[16,1,4096]{2,0,1:T(8,128)(2,1)S(1)} %all_gather.47, f32[4096]{0:T(1024)S(1)} %dynamic_slice.50, f32[16]{0:T(128)S(1)} %add_rsqrt_fusion), kind=kOutput, calls=%fused_computation.12 | convolution fusion | flops 235143168 | bytes 14942272 | tf_op jit(solution)/shard_map/dot_general | solution.py:153
  295.2 7.9 %fusion.5 = f32[16,1792]{1,0:T(8,128)} fusion(bf16[1,4096,1792]{2,1,0:T(8,128)(2,1)} %param.23, bf16[16,1,4096]{2,0,1:T(8,128)(2,1)S(1)} %all_gather.47, f32[4096]{0:T(1024)S(1)} %dynamic_slice.50, f32[16]{0:T(128)S(1)} %add_rsqrt_fusion), kind=kOutput, calls=%fused_computation.10 | convolution fusion | flops 235143168 | bytes 14942272 | tf_op jit(solution)/shard_map/dot_general | solution.py:156
  303.2 19.1 %all-reduce.6.cloned.1.call-done = (f32[16,1792]{1,0:T(8,128)}, f32[16,1792]{1,0:T(8,128)}) async-done(((f32[16,1792]{1,0:T(8,128)}, f32[16,1792]{1,0:T(8,128)}), (f32[16,1792]{1,0:T(8,128)}, f32[16,1792]{1,0:T(8,128)})) %all-reduce.6.cloned.1.call-update) | async-done | bytes 229392 | tf_op jit(solution)/shard_map/psum | solution.py:157
  322.4 8.0 %fusion.3 = f32[16,4096]{1,0:T(8,128)} fusion(bf16[1792,1,4096]{2,0,1:T(8,128)(2,1)} %param.24, f32[16,1792]{1,0:T(8,128)} %get-tuple-element.221, f32[16,1792]{1,0:T(8,128)} %get-tuple-element.222), kind=kOutput, calls=%fused_computation.8 | convolution fusion | flops 235053056 | bytes 15171584 | tf_op jit(solution)/shard_map/dot_general | solution.py:159
  330.4 72.4 %all-reduce.4.cloned.1.call-done = f32[16,4096]{1,0:T(8,128)} async-done(((f32[16,4096]{1,0:T(8,128)}), f32[16,4096]{1,0:T(8,128)}) %all-reduce.4.cloned.1.call-update) | async-done | bytes 262160 | tf_op jit(solution)/shard_map/psum | solution.py:162
  402.8 1.4 fusion.37
  (87 shorter events, 5.4 us)
Async XLA Ops:
  6.5 136.5 %copy-start = (bf16[8192,1,64]{0,2,1:T(8,128)(2,1)S(1)}, bf16[8192,1,64]{0,2,1:T(8,128)(2,1)}, u32[]{:S(2)}) copy-start(bf16[8192,1,64]{0,2,1:T(8,128)(2,1)} %param.18) | copy-start | bytes 3145732
  6.5 71.1 %copy-start.7 = (s32[16]{0:T(128)S(1)}, s32[16]{0:T(128)}, u32[]{:S(2)}) copy-start(s32[16]{0:T(128)} %param.27) | copy-start | bytes 196
  6.5 71.4 %copy-start.3 = (bf16[16,8,4,128]{3,2,1,0:T(4,128)(2,1)S(1)}, bf16[16,8,4,128]{3,2,1,0:T(4,128)(2,1)}, u32[]{:S(2)}) copy-start(bf16[16,8,4,128]{3,2,1,0:T(4,128)(2,1)} %param.25) | copy-start | bytes 393220
  6.5 71.8 %copy-start.4 = (bf16[16,8,4,128]{3,2,1,0:T(4,128)(2,1)S(1)}, bf16[16,8,4,128]{3,2,1,0:T(4,128)(2,1)}, u32[]{:S(2)}) copy-start(bf16[16,8,4,128]{3,2,1,0:T(4,128)(2,1)} %param.26) | copy-start | bytes 393220
  6.5 168.1 %copy-start.2 = (bf16[8192,1,64]{0,2,1:T(8,128)(2,1)S(1)}, bf16[8192,1,64]{0,2,1:T(8,128)(2,1)}, u32[]{:S(2)}) copy-start(bf16[8192,1,64]{0,2,1:T(8,128)(2,1)} %param.19) | copy-start | bytes 3145732
  6.5 219.9 %all-gather.7.cloned.1.call-start = ((), (), s32[]{:S(2)}) async-start(), calls=%async_computation.3 | async-start | bytes 2359296 | tf_op jit(solution)/shard_map/all_gather | solution.py:14
  79.7 173.3 %reduce-scatter.2.cloned.1.call-start = ((), (), s32[]{:S(2)}) async-start(), calls=%async_computation.1 | async-start | bytes 98304 | tf_op jit(solution)/shard_map/reduce_scatter | solution.py:143
  215.1 29.3 %copy-start.6 = (f32[8192]{0:T(1024)S(1)}, f32[8192]{0:T(1024)}, u32[]{:S(2)}) copy-start(f32[8192]{0:T(1024)} %param.21) | copy-start | bytes 98308
  215.1 37.9 %copy-start.5 = (bf16[16,1,512]{2,0,1:T(8,128)(2,1)S(1)}, bf16[16,1,512]{2,0,1:T(8,128)(2,1)}, u32[]{:S(2)}) copy-start(bf16[16,1,512]{2,0,1:T(8,128)(2,1)} %param.15) | copy-start | bytes 49156
  244.4 78.0 %all-reduce.6.cloned.1.call-start = ((), (), s32[]{:S(2)}) async-start(), calls=%async_computation.4 | async-start | bytes 458752 | tf_op jit(solution)/shard_map/psum | solution.py:157
  295.2 109.0 %copy-start.1 = (bf16[8192,1,64]{0,2,1:T(8,128)(2,1)S(1)}, bf16[8192,1,64]{0,2,1:T(8,128)(2,1)}, u32[]{:S(2)}) copy-start(bf16[8192,1,64]{0,2,1:T(8,128)(2,1)} %param.18) | copy-start | bytes 3145732
  303.2 99.6 %all-reduce.4.cloned.1.call-start = ((), (), s32[]{:S(2)}) async-start(), calls=%async_computation.2 | async-start | bytes 524288 | tf_op jit(solution)/shard_map/psum | solution.py:162
Sparse Core Ops, SparseCore 0:
  79.8 53.2 all-gather.6
  244.5 8.4 reduce-scatter.1
  303.3 19.0 all-reduce.5
  330.5 72.2 all-reduce.3
where the time goes:
time: 412 us; the launch traced here: 411 us
  blocking collectives  223 us (54%)
  waiting for transfers between devices  100 us (24%)
  matrix products  37.1 us (9%)
  local copies, waits for them, and re-layouts  24.6 us (6%)
  between operations  13.3 us (3%)
  other arithmetic  12.6 us (3%)
    psum x1, waiting for transfers between devices, per_device(): down_total = lax.psum(down_part, 'tp')  72.4 us
    all_gather x2, blocking collectives, joined(): gathered = jax.tree.map(lambda a: lax.all_gather(a, axis), part)  62.7 us
    all_gather x1, blocking collectives, spread_rows(): across = lax.all_gather(shard, 'tp', axis=2, tiled=True)  32.7 us
    all_gather x1, blocking collectives, half_rows_of(): return lax.all_gather(shard, 'tp', axis=2, tiled=True)  30.8 us
    all_gather x1, blocking collectives, per_device(): lax.all_gather(key_part, 'tp', axis=1, tiled=True)  30.6 us
    all_gather x1, blocking collectives, per_device(): lax.all_gather(value_part, 'tp', axis=1, tiled=True)  30.6 us
    all_gather x1, blocking collectives, per_device(): lax.all_gather(query_part, 'tp', axis=1, tiled=True)  30.5 us
    psum x1, waiting for transfers between devices, per_device(): gate_total, up_total = lax.psum((gate_part, up_part), 'sub')  19.1 us
  transfers between devices with their start and end apart: 4, of which 3 were waited for; matrix products, arithmetic and copies ran while one was open for 6% of the time, Pallas kernels for 0%

commit v1 on v0

--- a/solution.py
+++ b/solution.py
@@ -36,7 +36,14 @@
 
 
 def spread_rows(shard):
-    across = lax.all_gather(shard, "tp", axis=2, tiled=True)
+    size = lax.axis_size("tp")
+    right = [(i, (i + 1) % size) for i in range(size)]
+    shards = [shard]
+    for far in range(1, size):
+        shards = [lax.ppermute(shards[0], "tp", right), *shards]
+    full = jnp.concatenate(shards, axis=2)
+    shift = (lax.axis_index("tp") + 1) * shards[-1].shape[2]
+    across = jnp.roll(full, shift, axis=2)
     return lax.all_gather(across, "sub", axis=1, tiled=True)
 
 

time: 412 us -> 423 us (1.027)
  waiting for transfers between devices: 100 us -> 138 us
  blocking collectives: 223 us -> 189 us
    ppermute x0 -> x7, waiting for transfers between devices: none -> 41.3 us  [spread_rows(): shards = [lax.ppermute(shards[0], 'tp', right), *shards]]
    all_gather x1 -> x0, blocking collectives: 32.7 us -> none  [spread_rows(): across = lax.all_gather(shard, 'tp', axis=2, tiled=True)]
    unnamed x18 -> x31, local copies, waits for them, and re-layouts: 9.4 us -> 10.3 us
  transfers between devices with their start and end apart: 4 -> 11, of which waited for: 3 -> 10; matrix products, arithmetic and copies ran while one was open for 6% -> 6% of each run, Pallas kernels for 0% -> 0%
where the time goes in v1:
time: 423 us; the launch traced here: 422 us
  blocking collectives  189 us (45%)
  waiting for transfers between devices  138 us (33%)
  matrix products  37.1 us (9%)
  local copies, waits for them, and re-layouts  26.9 us (6%)
  other arithmetic  13.9 us (3%)
  between operations  13.4 us (3%)
    psum x1, waiting for transfers between devices, per_device(): down_total = lax.psum(down_part, 'tp')  72.4 us
    all_gather x2, blocking collectives, joined(): gathered = jax.tree.map(lambda a: lax.all_gather(a, axis), part)  61.6 us
    ppermute x7, waiting for transfers between devices, spread_rows(): shards = [lax.ppermute(shards[0], 'tp', right), *shards]  41.3 us
    all_gather x1, blocking collectives, per_device(): lax.all_gather(key_part, 'tp', axis=1, tiled=True)  31.1 us
    all_gather x1, blocking collectives, half_rows_of(): return lax.all_gather(shard, 'tp', axis=2, tiled=True)  30.8 us
    all_gather x1, blocking collectives, per_device(): lax.all_gather(value_part, 'tp', axis=1, tiled=True)  30.6 us
    all_gather x1, blocking collectives, per_device(): lax.all_gather(query_part, 'tp', axis=1, tiled=True)  30.6 us
    psum x1, waiting for transfers between devices, per_device(): gate_total, up_total = lax.psum((gate_part, up_part), 'sub')  19.1 us
  transfers between devices with their start and end apart: 11, of which 10 were waited for; matrix products, arithmetic and copies ran while one was open for 6% of the time, Pallas kernels for 0%

profile of v1, /device:TPU:0, one launch (start us, length us, event | category | flops | bytes accessed | tf_op | source)
XLA Modules:
  0.0 421.7 jit_solution(13579102507456587925)
XLA Ops:
  6.5 3.0 collective-permute-start
  9.6 5.0 %collective-permute-done = bf16[16,1,512]{2,0,1:T(8,128)(2,1)S(1)} collective-permute-done((bf16[16,1,512]{2,0,1:T(8,128)(2,1)}, bf16[16,1,512]{2,0,1:T(8,128)(2,1)S(1)}, u32[]{:S(2)}, u32[]{:S(2)}) %collective-permute-start) | collective-permute-done | bytes 16416 | tf_op jit(solution)/shard_map/ppermute | solution.py:43
  14.5 6.4 %collective-permute-done.1 = bf16[16,1,512]{2,0,1:T(8,128)(2,1)S(1)} collective-permute-done((bf16[16,1,512]{2,0,1:T(8,128)(2,1)S(1)}, bf16[16,1,512]{2,0,1:T(8,128)(2,1)S(1)}, u32[]{:S(2)}, u32[]{:S(2)}) %collective-permute-start.1) | collective-permute-done | bytes 16416 | tf_op jit(solution)/shard_map/ppermute | solution.py:43
  21.0 6.4 %collective-permute-done.2 = bf16[16,1,512]{2,0,1:T(8,128)(2,1)S(1)} collective-permute-done((bf16[16,1,512]{2,0,1:T(8,128)(2,1)S(1)}, bf16[16,1,512]{2,0,1:T(8,128)(2,1)S(1)}, u32[]{:S(2)}, u32[]{:S(2)}) %collective-permute-start.2) | collective-permute-done | bytes 16416 | tf_op jit(solution)/shard_map/ppermute | solution.py:43
  28.1 5.8 %collective-permute-done.3 = bf16[16,1,512]{2,0,1:T(8,128)(2,1)S(1)} collective-permute-done((bf16[16,1,512]{2,0,1:T(8,128)(2,1)S(1)}, bf16[16,1,512]{2,0,1:T(8,128)(2,1)S(1)}, u32[]{:S(2)}, u32[]{:S(2)}) %collective-permute-start.3) | collective-permute-done | bytes 16416 | tf_op jit(solution)/shard_map/ppermute | solution.py:43
  34.0 6.3 %collective-permute-done.4 = bf16[16,1,512]{2,0,1:T(8,128)(2,1)S(1)} collective-permute-done((bf16[16,1,512]{2,0,1:T(8,128)(2,1)S(1)}, bf16[16,1,512]{2,0,1:T(8,128)(2,1)S(1)}, u32[]{:S(2)}, u32[]{:S(2)}) %collective-permute-start.4) | collective-permute-done | bytes 16416 | tf_op jit(solution)/shard_map/ppermute | solution.py:43
  40.3 6.4 %collective-permute-done.5 = bf16[16,1,512]{2,0,1:T(8,128)(2,1)S(1)} collective-permute-done((bf16[16,1,512]{2,0,1:T(8,128)(2,1)S(1)}, bf16[16,1,512]{2,0,1:T(8,128)(2,1)S(1)}, u32[]{:S(2)}, u32[]{:S(2)}) %collective-permute-start.5) | collective-permute-done | bytes 16416 | tf_op jit(solution)/shard_map/ppermute | solution.py:43
  48.2 4.9 %collective-permute-done.6 = bf16[16,1,512]{2,0,1:T(8,128)(2,1)S(1)} collective-permute-done((bf16[16,1,512]{2,0,1:T(8,128)(2,1)S(1)}, bf16[16,1,512]{2,0,1:T(8,128)(2,1)S(1)}, u32[]{:S(2)}, u32[]{:S(2)}) %collective-permute-start.6) | collective-permute-done | bytes 16416 | tf_op jit(solution)/shard_map/ppermute | solution.py:43
  54.7 2.0 all_gather.33
  57.1 4.6 %fusion.12 = bf16[16,512]{1,0:T(8,128)(2,1)S(1)} fusion(bf16[16,8192]{1,0:T(8,128)(2,1)S(1)} %bitcast.90, bf16[8192,1,512]{2,0,1:T(8,128)(2,1)} %param.17), kind=kOutput, calls=%fused_computation.18 | convolution fusion | flops 134225920 | bytes 8667136 | tf_op jit(solution)/shard_map/dot_general | solution.py:92
  61.7 30.6 %all_gather.34 = bf16[16,4096]{1,0:T(8,128)(2,1)S(1)} all-gather(bf16[16,512]{1,0:T(8,128)(2,1)S(1)} %fusion.12), channel_id=1, replica_groups=mesh['grp'=2,'tp'=8,'sub'=2] {'tp'}, dimensions={1}, use_global_device_ids=true | all-gather | bytes 147456 | tf_op jit(solution)/shard_map/all_gather | solution.py:102
  92.8 1.3 fusion.26
  94.2 9.4 %copy.83 = bf16[512,8,2,512]{3,1,2,0:T(8,128)(2,1)} copy(bf16[512,8,2,512]{3,2,1,0:T(2,128)(2,1)} %bitcast.89) | data formatting | bytes 16777216
  103.6 12.0 %copy.75 = bf16[1024,4096]{1,0:T(8,128)(2,1)} copy(bf16[1024,4096]{0,1:T(8,128)(2,1)} %bitcast.88) | data formatting | bytes 16777216 | tf_op jit(solution)/shard_map/dot_general | solution.py:146
  116.1 31.1 %all-gather.3 = bf16[8,64,16]{1,2,0:T(8,128)(2,1)S(1)} all-gather(bf16[1,64,16]{1,2,0:T(8,128)(2,1)S(1)} %fusion.15), channel_id=1, replica_groups=mesh['grp'=2,'tp'=8,'sub'=2] {'tp'}, dimensions={0}, use_global_device_ids=true | all-gather | bytes 18432 | tf_op jit(solution)/shard_map/all_gather | solution.py:103
  147.9 30.9 %all-gather.1 = f32[128,4,8]{2,1,0:T(4,128)S(1)} all-gather(f32[16,4,8]{2,1,0:T(4,128)S(1)} %fusion.27), channel_id=3, replica_groups=mesh['grp'=2,'tp'=8,'sub'=2] {'tp'}, dimensions={0}, use_global_device_ids=true | all-gather | bytes 18432 | tf_op jit(solution)/shard_map/all_gather | solution.py:14
  179.0 30.7 %all-gather = f32[128,4,8]{2,1,0:T(4,128)S(1)} all-gather(f32[16,4,8]{2,1,0:T(4,128)S(1)} %get-tuple-element.236), channel_id=2, replica_groups=mesh['grp'=2,'tp'=8,'sub'=2] {'tp'}, dimensions={0}, use_global_device_ids=true | all-gather | bytes 18432 | tf_op jit(solution)/shard_map/all_gather | solution.py:14
  210.4 30.6 %all-gather.4 = bf16[8,64,16]{1,2,0:T(8,128)(2,1)S(1)} all-gather(bf16[1,64,16]{1,2,0:T(8,128)(2,1)S(1)} %fusion.16), channel_id=1, replica_groups=mesh['grp'=2,'tp'=8,'sub'=2] {'tp'}, dimensions={0}, use_global_device_ids=true | all-gather | bytes 18432 | tf_op jit(solution)/shard_map/all_gather | solution.py:104
  242.1 10.0 %while.19 = (s32[]{:T(128)}, f32[16,4,8]{0,2,1:T(8,128)S(1)}, f32[16,4,8]{0,2,1:T(8,128)S(1)}, f32[16,4,8,128]{3,2,1,0:T(8,128)S(1)}, f32[8,16,4,8]{1,3,2,0:T(8,...) while((s32[]{:T(128)}, f32[16,4,8]{0,2,1:T(8,128)S(1)}, ...), condition=%wide.region_4.5_spmd, body=%wide.region_3.4_spmd.sunk | while | flops 199685 | bytes 815255 | solution.py:19
  242.3 1.2 fusion.58
  246.6 1.2 fusion.58
  248.0 1.2 fusion.58
  252.7 6.3 %fusion.49 = f32[16,2,512]{2,0,1:T(8,128)} fusion(bf16[16,4096,1]{1,0,2:T(8,128)(2,1)S(1)} %reshape.198, bf16[2,512,4096]{2,1,0:T(8,128)(2,1)} %bitcast.87), kind=kOutput, calls=%fused_computation.94 | convolution fusion | flops 134217728 | bytes 8585216 | tf_op jit(solution)/shard_map/dot_general | solution.py:146
  259.1 4.8 %reduce-scatter.2.cloned.1.call-done = f32[16,1,512]{2,0,1:T(8,128)} async-done(((f32[16,2,512]{2,0,1:T(8,128)}), f32[16,1,512]{2,0,1:T(8,128)}) %reduce-scatter.2.cloned.1.call-update) | async-done | bytes 32784 | tf_op jit(solution)/shard_map/reduce_scatter | solution.py:150
  264.7 30.8 %all_gather.43 = bf16[16,1,4096]{2,0,1:T(8,128)(2,1)S(1)} all-gather(bf16[16,1,512]{2,0,1:T(8,128)(2,1)S(1)} %add_convert_fusion.1), channel_id=1, replica_groups=mesh['grp'=2,'tp'=8,'sub'=2] {'tp'}, dimensions={2}, use_global_device_ids=true | all-gather | bytes 147456 | tf_op jit(solution)/shard_map/all_gather | solution.py:51
  295.6 2.6 psum.28
  298.3 7.9 %fusion.7 = f32[16,1792]{1,0:T(8,128)} fusion(bf16[1,4096,1792]{2,1,0:T(8,128)(2,1)} %param.22, bf16[16,1,4096]{2,0,1:T(8,128)(2,1)S(1)} %all_gather.43, f32[4096]{0:T(1024)S(1)} %dynamic_slice.55, f32[16]{0:T(128)S(1)} %add_rsqrt_fusion), kind=kOutput, calls=%fused_computation.12 | convolution fusion | flops 235143168 | bytes 14942272 | tf_op jit(solution)/shard_map/dot_general | solution.py:160
  306.1 8.0 %fusion.5 = f32[16,1792]{1,0:T(8,128)} fusion(bf16[1,4096,1792]{2,1,0:T(8,128)(2,1)} %param.23, bf16[16,1,4096]{2,0,1:T(8,128)(2,1)S(1)} %all_gather.43, f32[4096]{0:T(1024)S(1)} %dynamic_slice.55, f32[16]{0:T(128)S(1)} %add_rsqrt_fusion), kind=kOutput, calls=%fused_computation.10 | convolution fusion | flops 235143168 | bytes 14942272 | tf_op jit(solution)/shard_map/dot_general | solution.py:163
  314.2 19.1 %all-reduce.6.cloned.1.call-done = (f32[16,1792]{1,0:T(8,128)}, f32[16,1792]{1,0:T(8,128)}) async-done(((f32[16,1792]{1,0:T(8,128)}, f32[16,1792]{1,0:T(8,128)}), (f32[16,1792]{1,0:T(8,128)}, f32[16,1792]{1,0:T(8,128)})) %all-reduce.6.cloned.1.call-update) | async-done | bytes 229392 | tf_op jit(solution)/shard_map/psum | solution.py:164
  333.3 8.0 %fusion.3 = f32[16,4096]{1,0:T(8,128)} fusion(bf16[1792,1,4096]{2,0,1:T(8,128)(2,1)} %param.24, f32[16,1792]{1,0:T(8,128)} %get-tuple-element.221, f32[16,1792]{1,0:T(8,128)} %get-tuple-element.222), kind=kOutput, calls=%fused_computation.8 | convolution fusion | flops 235053056 | bytes 15171584 | tf_op jit(solution)/shard_map/dot_general | solution.py:166
  341.4 72.4 %all-reduce.4.cloned.1.call-done = f32[16,4096]{1,0:T(8,128)} async-done(((f32[16,4096]{1,0:T(8,128)}), f32[16,4096]{1,0:T(8,128)}) %all-reduce.4.cloned.1.call-update) | async-done | bytes 262160 | tf_op jit(solution)/shard_map/psum | solution.py:169
  413.8 1.4 fusion.37
  (115 shorter events, 15.6 us)
Async XLA Ops:
  6.5 109.1 %copy-start = (bf16[8192,1,64]{0,2,1:T(8,128)(2,1)S(1)}, bf16[8192,1,64]{0,2,1:T(8,128)(2,1)}, u32[]{:S(2)}) copy-start(bf16[8192,1,64]{0,2,1:T(8,128)(2,1)} %param.18) | copy-start | bytes 3145732
  6.5 85.9 %copy-start.4 = (bf16[16,8,4,128]{3,2,1,0:T(4,128)(2,1)S(1)}, bf16[16,8,4,128]{3,2,1,0:T(4,128)(2,1)}, u32[]{:S(2)}) copy-start(bf16[16,8,4,128]{3,2,1,0:T(4,128)(2,1)} %param.25) | copy-start | bytes 393220
  6.5 86.3 %copy-start.5 = (bf16[16,8,4,128]{3,2,1,0:T(4,128)(2,1)S(1)}, bf16[16,8,4,128]{3,2,1,0:T(4,128)(2,1)}, u32[]{:S(2)}) copy-start(bf16[16,8,4,128]{3,2,1,0:T(4,128)(2,1)} %param.26) | copy-start | bytes 393220
  6.5 234.6 %all-gather.7.cloned.1.call-start = ((), (), s32[]{:S(2)}) async-start(), calls=%async_computation.3 | async-start | bytes 2359296 | tf_op jit(solution)/shard_map/all_gather | solution.py:14
  6.5 8.0 %collective-permute-start = (bf16[16,1,512]{2,0,1:T(8,128)(2,1)}, bf16[16,1,512]{2,0,1:T(8,128)(2,1)S(1)}, u32[]{:S(2)}, u32[]{:S(2)}) collective-permute-start(bf16[16,1,512]{2,0,1:T(8,128)(2,1)} %param.15), channel_id=1, source_target_pairs={{0,2},{2,4},{4,6},{6,8},{8,10},{10,12},{12,14},{14,0},{1,3},{3,5},... | collective-permute-start | bytes 49160 | tf_op jit(solution)/shard_map/ppermute | solution.py:43
  14.5 6.4 %collective-permute-start.1 = (bf16[16,1,512]{2,0,1:T(8,128)(2,1)S(1)}, bf16[16,1,512]{2,0,1:T(8,128)(2,1)S(1)}, u32[]{:S(2)}, u32[]{:S(2)}) collective-permute-start(bf16[16,1,512]{2,0,1:T(8,128)(2,1)S(1)} %collective-permute-done), channel_id=1, source_target_pairs={{0,2},{2,4},{4,6},{6,8},{8,10},{10,12},{12,14},{14,0},{1,3},{3,5},... | collective-permute-start | bytes 49160 | tf_op jit(solution)/shard_map/ppermute | solution.py:43
  21.0 6.4 %collective-permute-start.2 = (bf16[16,1,512]{2,0,1:T(8,128)(2,1)S(1)}, bf16[16,1,512]{2,0,1:T(8,128)(2,1)S(1)}, u32[]{:S(2)}, u32[]{:S(2)}) collective-permute-start(bf16[16,1,512]{2,0,1:T(8,128)(2,1)S(1)} %collective-permute-done.1), channel_id=1, source_target_pairs={{0,2},{2,4},{4,6},{6,8},{8,10},{10,12},{12,14},{14,0},{1,3},{3,5},... | collective-permute-start | bytes 49160 | tf_op jit(solution)/shard_map/ppermute | solution.py:43
  27.4 6.4 %collective-permute-start.3 = (bf16[16,1,512]{2,0,1:T(8,128)(2,1)S(1)}, bf16[16,1,512]{2,0,1:T(8,128)(2,1)S(1)}, u32[]{:S(2)}, u32[]{:S(2)}) collective-permute-start(bf16[16,1,512]{2,0,1:T(8,128)(2,1)S(1)} %collective-permute-done.2), channel_id=1, source_target_pairs={{0,2},{2,4},{4,6},{6,8},{8,10},{10,12},{12,14},{14,0},{1,3},{3,5},... | collective-permute-start | bytes 49160 | tf_op jit(solution)/shard_map/ppermute | solution.py:43
  33.8 6.4 %collective-permute-start.4 = (bf16[16,1,512]{2,0,1:T(8,128)(2,1)S(1)}, bf16[16,1,512]{2,0,1:T(8,128)(2,1)S(1)}, u32[]{:S(2)}, u32[]{:S(2)}) collective-permute-start(bf16[16,1,512]{2,0,1:T(8,128)(2,1)S(1)} %collective-permute-done.3), channel_id=1, source_target_pairs={{0,2},{2,4},{4,6},{6,8},{8,10},{10,12},{12,14},{14,0},{1,3},{3,5},... | collective-permute-start | bytes 49160 | tf_op jit(solution)/shard_map/ppermute | solution.py:43
  40.3 6.4 %collective-permute-start.5 = (bf16[16,1,512]{2,0,1:T(8,128)(2,1)S(1)}, bf16[16,1,512]{2,0,1:T(8,128)(2,1)S(1)}, u32[]{:S(2)}, u32[]{:S(2)}) collective-permute-start(bf16[16,1,512]{2,0,1:T(8,128)(2,1)S(1)} %collective-permute-done.4), channel_id=1, source_target_pairs={{0,2},{2,4},{4,6},{6,8},{8,10},{10,12},{12,14},{14,0},{1,3},{3,5},... | collective-permute-start | bytes 49160 | tf_op jit(solution)/shard_map/ppermute | solution.py:43
  46.7 6.4 %collective-permute-start.6 = (bf16[16,1,512]{2,0,1:T(8,128)(2,1)S(1)}, bf16[16,1,512]{2,0,1:T(8,128)(2,1)S(1)}, u32[]{:S(2)}, u32[]{:S(2)}) collective-permute-start(bf16[16,1,512]{2,0,1:T(8,128)(2,1)S(1)} %collective-permute-done.5), channel_id=1, source_target_pairs={{0,2},{2,4},{4,6},{6,8},{8,10},{10,12},{12,14},{14,0},{1,3},{3,5},... | collective-permute-start | bytes 49160 | tf_op jit(solution)/shard_map/ppermute | solution.py:43
  94.1 169.8 %reduce-scatter.2.cloned.1.call-start = ((), (), s32[]{:S(2)}) async-start(), calls=%async_computation.1 | async-start | bytes 98304 | tf_op jit(solution)/shard_map/reduce_scatter | solution.py:150
  94.2 115.8 %copy-start.2 = (bf16[8192,1,64]{0,2,1:T(8,128)(2,1)S(1)}, bf16[8192,1,64]{0,2,1:T(8,128)(2,1)}, u32[]{:S(2)}) copy-start(bf16[8192,1,64]{0,2,1:T(8,128)(2,1)} %param.19) | copy-start | bytes 3145732
  115.7 143.4 %copy-start.6 = (f32[8192]{0:T(1024)S(1)}, f32[8192]{0:T(1024)}, u32[]{:S(2)}) copy-start(f32[8192]{0:T(1024)} %param.21) | copy-start | bytes 98308
  115.7 148.3 %copy-start.3 = (bf16[16,1,512]{2,0,1:T(8,128)(2,1)S(1)}, bf16[16,1,512]{2,0,1:T(8,128)(2,1)}, u32[]{:S(2)}) copy-start(bf16[16,1,512]{2,0,1:T(8,128)(2,1)} %param.15) | copy-start | bytes 49156
  259.0 74.3 %all-reduce.6.cloned.1.call-start = ((), (), s32[]{:S(2)}) async-start(), calls=%async_computation.4 | async-start | bytes 458752 | tf_op jit(solution)/shard_map/psum | solution.py:164
  306.1 109.0 %copy-start.1 = (bf16[8192,1,64]{0,2,1:T(8,128)(2,1)S(1)}, bf16[8192,1,64]{0,2,1:T(8,128)(2,1)}, u32[]{:S(2)}) copy-start(bf16[8192,1,64]{0,2,1:T(8,128)(2,1)} %param.18) | copy-start | bytes 3145732
  314.1 99.6 %all-reduce.4.cloned.1.call-start = ((), (), s32[]{:S(2)}) async-start(), calls=%async_computation.2 | async-start | bytes 524288 | tf_op jit(solution)/shard_map/psum | solution.py:169
Sparse Core Ops, SparseCore 0:
  94.3 47.1 all-gather.6
  259.1 4.7 reduce-scatter.1
  314.2 19.0 all-reduce.5
  341.5 72.2 all-reduce.3
